TPU v7x, 32 devices: a whole 2x2x4 slice. The times are simulated.
32 devices in a mesh: lat: 8 (over y, x, core), lon: 4 (over z).
Axes of the slice: x: 2, y: 2, z: 4, core: 2. Of those that a mesh axis runs over, the one named last changes fastest.
Arguments:
- current: bfloat16 [69, 256, 512], P(None, 'lat', 'lon')
- next_fields: bfloat16 [96, 256, 512], P(('lat', 'lon')), may hold values from -6 to 6
- reader_slot: int32 [69], replicated, may hold values from 0 to 95, as said below
- first_weight: bfloat16 [9, 256, 69], replicated, may hold values from -0.25 to 0.25
- first_bias: float32 [256], replicated, may hold values from -3 to 3
- second_weight: bfloat16 [9, 256, 256], replicated, may hold values from -0.125 to 0.125
- second_bias: float32 [256], replicated, may hold values from -3 to 3
Outputs:
- features: bfloat16 [256, 256, 512], P(None, 'lat', 'lon')
- next_tile: bfloat16 [69, 256, 512], P(None, 'lat', 'lon')
Inputs may be any that keep to these rules, and one draw needn't show every extreme that they name: `reader_slot`: the 69 entries are different slots.
All inputs are finite; a program needn't handle non-finite values.
Results may differ from a plain program's by a relative error of at most 0.0053.
Values may be sent and summed in bfloat16 or wider, within the bound.
A program may use at most 128 MiB of HBM per device.

v0:
```python
import jax
import jax.numpy as jnp
from jax import lax
from jax.sharding import PartitionSpec as P


def padded_2(block, sides, width, periodic):
    for axis, dim in sides:
        count = lax.axis_size(axis)
        forward = [(i, i + 1) for i in range(count - 1)]
        if periodic:
            forward.append((count - 1, 0))
        backward = [(target, source) for source, target in forward]
        low = lax.ppermute(
            lax.slice_in_dim(block, block.shape[dim] - width, None, axis=dim), axis, forward
        )
        high = lax.ppermute(lax.slice_in_dim(block, 0, width, axis=dim), axis, backward)
        block = jnp.concatenate([low, block, high], axis=dim)
    return block


def conv_valid(padded, weight, bias):
    rows = padded.shape[1] - 2
    cols = padded.shape[2] - 2
    total = jnp.zeros((weight.shape[1], rows, cols), jnp.float32)
    for tap in range(9):
        shifted = padded[:, tap // 3 : tap // 3 + rows, tap % 3 : tap % 3 + cols]
        total = total + jnp.einsum(
            "ok,khw->ohw", weight[tap], shifted, preferred_element_type=jnp.float32
        )
    return total + bias[:, None, None]


def regrid(next_fields, reader_slot):
    slot_dev, rows_all, cols_all = next_fields.shape
    n_lat = lax.axis_size("lat")
    n_lon = lax.axis_size("lon")
    lat_rows = rows_all // n_lat
    lon_cols = cols_all // n_lon
    blocks = next_fields.reshape(slot_dev, n_lat, lat_rows, n_lon, lon_cols)
    ordered = blocks.transpose(1, 3, 0, 2, 4).reshape(n_lat * n_lon, slot_dev, lat_rows, lon_cols)
    moved = lax.all_to_all(ordered, ("lat", "lon"), split_axis=0, concat_axis=1, tiled=True)
    moved = moved.reshape(n_lat * n_lon * slot_dev, lat_rows, lon_cols)
    return jnp.take(moved, reader_slot, axis=0)


def encode(current, first_weight, first_bias, second_weight, second_bias):
    values = current.astype(jnp.float32)
    lat_rows = values.shape[1]
    lon_cols = values.shape[2]
    cells = lat_rows * lax.axis_size("lat") * lon_cols * lax.axis_size("lon")
    total, squares = lax.psum(
        (jnp.sum(values, axis=(1, 2)), jnp.sum(values * values, axis=(1, 2))), ("lat", "lon")
    )
    mean = total / cells
    scale = 1.0 / jnp.sqrt(squares / cells - mean * mean + 1e-05)
    normed = ((values - mean[:, None, None]) * scale[:, None, None]).astype(jnp.bfloat16)
    tall = padded_2(normed, (("lat", 1),), 2, False)
    padded = padded_2(tall, (("lon", 2),), 2, True)
    hidden = jax.nn.gelu(conv_valid(padded, first_weight, first_bias), approximate=True)
    global_row = lax.axis_index("lat") * lat_rows + jnp.arange(lat_rows + 2, dtype=jnp.int32) - 1
    inside = (global_row >= 0) & (global_row < lat_rows * lax.axis_size("lat"))
    hidden = jnp.where(inside[None, :, None], hidden, 0.0).astype(jnp.bfloat16)
    return conv_valid(hidden, second_weight, second_bias).astype(jnp.bfloat16)


def body(current, next_fields, reader_slot, first_weight, first_bias, second_weight, second_bias):
    features = encode(current, first_weight, first_bias, second_weight, second_bias)
    next_tile = regrid(next_fields, reader_slot)
    return (features, next_tile)


def solution(mesh):
    in_specs = (P(None, "lat", "lon"), P(("lat", "lon"), None, None), P(), P(), P(), P(), P())
    out_specs = (P(None, "lat", "lon"), P(None, "lat", "lon"))
    return jax.shard_map(body, mesh=mesh, in_specs=in_specs, out_specs=out_specs, check_vma=False)
```

profile of v0, /device:TPU:8, one launch (start us, length us, event | category | flops | bytes accessed | tf_op | source)
XLA Modules:
  0.0 147.3 jit_solution(17535352118714095713)
XLA Ops:
  0.6 0.0 copy-start.1
  0.6 1.8 %copy.13 = bf16[69,32,128]{0,2,1:T(8,128)(2,1)S(1)} copy(bf16[69,32,128]{2,1,0:T(8,128)(2,1)} %param.7) | data formatting | bytes 1130496 | tf_op args[0]
  2.5 0.6 convert_reduce_fusion
  3.1 40.4 %all-reduce = (f32[69]{0:T(128)S(1)}, f32[69]{0:T(128)S(1)}) all-reduce(f32[69]{0:T(128)S(1)} %get-tuple-element.9, f32[69]{0:T(128)S(1)} %get-tuple-element.8), channel_id=1, replica_groups=mesh['lat'=8,'lon'=4] {'lat','lon'}, use_global_device_ids=true, to_apply=%region_3.0 | all-reduce | flops 138 | bytes 1104 | tf_op jit(solution)/shard_map/psum | solution.py:52
  43.5 0.3 fusion.10
  43.8 0.0 copy-start.5
  43.9 1.3 collective-permute-start
  45.2 1.3 collective-permute-start.1
  46.5 0.0 copy-done.1
  46.5 0.2 reshape.34
  46.7 1.1 copy.14
  47.7 0.0 copy-start.2
  47.7 8.6 %all-to-all-start = ((bf16[32,3,32,128]{3,2,1,0:T(8,128)(2,1)}), bf16[32,3,32,128]{3,2,1,0:T(8,128)(2,1)}, u32[]{:S(2)}, u32[]{:S(2)}) async-start(bf16[32,3,32,128]{3,2,1,0:T(8,128)(2,1)} %bitcast.39), calls=%async_computation | async-start | bytes 1572864 | tf_op jit(solution)/shard_map/all_to_all | solution.py:42
  56.3 0.0 copy-done.5
  56.4 0.0 collective-permute-done
  56.4 0.0 collective-permute-done.1
  56.5 0.4 collective-permute-start.3
  56.8 1.7 %collective-permute-start.2 = (bf16[69,36,2]{0,2,1:T(2,128)(2,1)S(1)}, bf16[69,36,2]{0,2,1:T(2,128)(2,1)S(1)}, u32[]{:S(2)}, u32[]{:S(2)}) collective-permute-start(bf16[69,36,2]{0,2,1:T(2,128)(2,1)S(1)} %get-tuple-element.12), channel_id=1, source_target_pairs={{0,1},{1,2},{2,3},{3,0},{4,5},{5,6},{6,7},{7,4},{8,9},{9,10},{10,1... | collective-permute-start | bytes 29816 | tf_op jit(solution)/shard_map/ppermute | solution.py:14
  58.5 17.9 %collective-permute-done.3 = bf16[69,36,2]{0,2,1:T(2,128)(2,1)S(1)} collective-permute-done((bf16[69,36,2]{0,2,1:T(2,128)(2,1)S(1)}, bf16[69,36,2]{0,2,1:T(2,128)(2,1)S(1)}, u32[]{:S(2)}, u32[]{:S(2)}) %collective-permute-start.3) | collective-permute-done | bytes 9968 | tf_op jit(solution)/shard_map/ppermute | solution.py:17
  76.4 0.0 collective-permute-done.2
  76.4 0.5 pad_maximum_fusion
  76.9 0.0 copy-done.2
  76.9 0.8 fusion.32
  77.7 3.0 %fusion.34 = f32[34,130,256]{2,1,0:T(8,128)} fusion(bf16[69,36,132]{0,2,1:T(8,128)(2,1)S(1)} %pad_maximum_fusion, bf16[9,256,69]{1,2,0:T(8,128)(2,1)S(1)} %copy-done.2), kind=kOutput, calls=%fused_computation.41 | convolution fusion | flops 156149760 | bytes 5746688 | tf_op jit(solution)/shard_map/ok,khw->ohw/dot_general | solution.py:28
  80.7 2.9 %fusion.36 = f32[34,130,256]{2,1,0:T(8,128)} fusion(bf16[69,36,132]{0,2,1:T(8,128)(2,1)S(1)} %pad_maximum_fusion, bf16[9,256,69]{1,2,0:T(8,128)(2,1)S(1)} %copy-done.2), kind=kOutput, calls=%fused_computation.43 | convolution fusion | flops 156149760 | bytes 5746688 | tf_op jit(solution)/shard_map/ok,khw->ohw/dot_general | solution.py:28
  83.6 2.9 %fusion.63 = f32[34,130,256]{2,1,0:T(8,128)} fusion(bf16[9,256,69]{1,2,0:T(8,128)(2,1)S(1)} %copy-done.2, bf16[69,36,2]{0,2,1:T(2,128)(2,1)S(1)} %collective-permute-done.3, bf16[69,2,128]{0,2,1:T(8,128)(2,1)S(1)} %collective-permute-done.1, bf16[69,32,128]{0,2,1:T(8,128)(2,1)S(1)} %fusion.10, bf16[69,2,128]{0,2,1:T(8,128)(2,1)S(1)} %collective-permute-done), kind=kOutput, calls=%fused_computation.69 | convolution fusion | flops 158733120 | bytes 5761024 | tf_op jit(solution)/shard_map/ok,khw->ohw/dot_general | solution.py:28
  86.5 2.9 %fusion.66 = f32[34,130,256]{2,1,0:T(8,128)} fusion(bf16[9,256,69]{1,2,0:T(8,128)(2,1)S(1)} %copy-done.2, bf16[69,2,128]{0,2,1:T(8,128)(2,1)S(1)} %collective-permute-done.1, bf16[69,32,128]{0,2,1:T(8,128)(2,1)S(1)} %fusion.10, bf16[69,2,128]{0,2,1:T(8,128)(2,1)S(1)} %collective-permute-done, bf16[69,36,2]{0,2,1:T(2,128)(2,1)S(1)} %collective-permute-done.2), kind=kOutput, calls=%fused_computation.72 | convolution fusion | flops 158733120 | bytes 5761024 | tf_op jit(solution)/shard_map/ok,khw->ohw/dot_general | solution.py:28
  89.4 3.0 %fusion.68 = f32[34,130,256]{2,1,0:T(8,128)} fusion(bf16[9,256,69]{1,2,0:T(8,128)(2,1)S(1)} %copy-done.2, bf16[69,36,2]{0,2,1:T(2,128)(2,1)S(1)} %collective-permute-done.3, bf16[69,2,128]{0,2,1:T(8,128)(2,1)S(1)} %collective-permute-done.1, bf16[69,32,128]{0,2,1:T(8,128)(2,1)S(1)} %fusion.10, bf16[69,2,128]{0,2,1:T(8,128)(2,1)S(1)} %collective-permute-done), kind=kOutput, calls=%fused_computation.74 | convolution fusion | flops 158733120 | bytes 5761024 | tf_op jit(solution)/shard_map/ok,khw->ohw/dot_general | solution.py:28
  92.4 3.0 %fusion.71 = f32[34,130,256]{2,1,0:T(8,128)} fusion(bf16[9,256,69]{1,2,0:T(8,128)(2,1)S(1)} %copy-done.2, bf16[69,2,128]{0,2,1:T(8,128)(2,1)S(1)} %collective-permute-done.1, bf16[69,32,128]{0,2,1:T(8,128)(2,1)S(1)} %fusion.10, bf16[69,2,128]{0,2,1:T(8,128)(2,1)S(1)} %collective-permute-done, bf16[69,36,2]{0,2,1:T(2,128)(2,1)S(1)} %collective-permute-done.2), kind=kOutput, calls=%fused_computation.77 | convolution fusion | flops 158733120 | bytes 5761024 | tf_op jit(solution)/shard_map/ok,khw->ohw/dot_general | solution.py:28
  95.4 0.0 copy-start.3
  95.4 2.9 %fusion.61 = f32[34,130,256]{2,1,0:T(8,128)} fusion(bf16[9,256,69]{1,2,0:T(8,128)(2,1)S(1)} %copy-done.2, bf16[69,2,128]{0,2,1:T(8,128)(2,1)S(1)} %collective-permute-done.1, bf16[69,32,128]{0,2,1:T(8,128)(2,1)S(1)} %fusion.10, bf16[69,2,128]{0,2,1:T(8,128)(2,1)S(1)} %collective-permute-done, bf16[69,36,2]{0,2,1:T(2,128)(2,1)S(1)} %collective-permute-done.2), kind=kOutput, calls=%fused_computation.67 | convolution fusion | flops 158733120 | bytes 5761024 | tf_op jit(solution)/shard_map/ok,khw->ohw/dot_general | solution.py:28
  98.3 0.0 copy-done.3
  98.3 0.0 copy-start
  98.3 12.7 %fusion.8 = bf16[256,34,130]{0,2,1:T(8,128)(2,1)S(1)} fusion(f32[34,130,256]{2,1,0:T(8,128)S(1)} %fusion.32, f32[34,130,256]{2,1,0:T(8,128)} %fusion.61, f32[34,130,256]{2,1,0:T(8,128)} %fusion.63, f32[34,130,256]{2,1,0:T(8,128)} %fusion.34, f32[34,130,256]{2,1,0:T(8,128)} %fusion.66, f32[34,130,256]{2,1,0:T(8,128)} %fusion.68, ...), kind=kOutput, calls=%fused_computation.10 | convolution fusion | flops 180232000 | bytes 39917056 | tf_op jit(solution)/shard_map/ok,khw->ohw/dot_general | solution.py:28
  111.0 0.0 copy-done
  111.0 0.8 fusion.13
  111.7 2.7 %fusion.15 = f32[32,128,256]{2,1,0:T(8,128)} fusion(bf16[256,34,130]{0,2,1:T(8,128)(2,1)S(1)} %fusion.8, bf16[9,256,256]{2,1,0:T(8,128)(2,1)S(1)} %copy-done), kind=kOutput, calls=%fused_computation.21 | convolution fusion | flops 536870912 | bytes 6422528 | tf_op jit(solution)/shard_map/ok,khw->ohw/dot_general | solution.py:28
  114.4 2.7 %fusion.17 = f32[32,128,256]{2,1,0:T(8,128)} fusion(bf16[256,34,130]{0,2,1:T(8,128)(2,1)S(1)} %fusion.8, bf16[9,256,256]{2,1,0:T(8,128)(2,1)S(1)} %copy-done), kind=kOutput, calls=%fused_computation.23 | convolution fusion | flops 536870912 | bytes 6422528 | tf_op jit(solution)/shard_map/ok,khw->ohw/dot_general | solution.py:28
  117.2 2.7 %fusion.19 = f32[32,128,256]{2,1,0:T(8,128)} fusion(bf16[256,34,130]{0,2,1:T(8,128)(2,1)S(1)} %fusion.8, bf16[9,256,256]{2,1,0:T(8,128)(2,1)S(1)} %copy-done), kind=kOutput, calls=%fused_computation.25 | convolution fusion | flops 536870912 | bytes 6422528 | tf_op jit(solution)/shard_map/ok,khw->ohw/dot_general | solution.py:28
  119.9 2.7 %fusion.21 = f32[32,128,256]{2,1,0:T(8,128)} fusion(bf16[256,34,130]{0,2,1:T(8,128)(2,1)S(1)} %fusion.8, bf16[9,256,256]{2,1,0:T(8,128)(2,1)S(1)} %copy-done), kind=kOutput, calls=%fused_computation.27 | convolution fusion | flops 536870912 | bytes 6422528 | tf_op jit(solution)/shard_map/ok,khw->ohw/dot_general | solution.py:28
  122.6 2.7 %fusion.23 = f32[32,128,256]{2,1,0:T(8,128)} fusion(bf16[256,34,130]{0,2,1:T(8,128)(2,1)S(1)} %fusion.8, bf16[9,256,256]{2,1,0:T(8,128)(2,1)S(1)} %copy-done), kind=kOutput, calls=%fused_computation.29 | convolution fusion | flops 536870912 | bytes 6422528 | tf_op jit(solution)/shard_map/ok,khw->ohw/dot_general | solution.py:28
  125.3 2.7 %fusion.25 = f32[32,128,256]{2,1,0:T(8,128)} fusion(bf16[256,34,130]{0,2,1:T(8,128)(2,1)S(1)} %fusion.8, bf16[9,256,256]{2,1,0:T(8,128)(2,1)S(1)} %copy-done), kind=kOutput, calls=%fused_computation.31 | convolution fusion | flops 536870912 | bytes 6422528 | tf_op jit(solution)/shard_map/ok,khw->ohw/dot_general | solution.py:28
  128.0 0.0 copy-start.4
  128.0 2.7 %fusion.27 = f32[32,128,256]{2,1,0:T(8,128)} fusion(bf16[256,34,130]{0,2,1:T(8,128)(2,1)S(1)} %fusion.8, bf16[9,256,256]{2,1,0:T(8,128)(2,1)S(1)} %copy-done), kind=kOutput, calls=%fused_computation.33 | convolution fusion | flops 536870912 | bytes 6422528 | tf_op jit(solution)/shard_map/ok,khw->ohw/dot_general | solution.py:28
  130.7 0.0 copy-done.4
  130.7 10.8 %fusion.29 = bf16[256,32,128]{0,2,1:T(8,128)(2,1)S(1)} fusion(f32[256]{0:T(256)S(1)} %copy-done.4, bf16[256,34,130]{0,2,1:T(8,128)(2,1)S(1)} %fusion.8, f32[32,128,256]{2,1,0:T(8,128)S(1)} %fusion.13, f32[32,128,256]{2,1,0:T(8,128)} %fusion.15, f32[32,128,256]{2,1,0:T(8,128)} %fusion.17, f32[32,128,256]{2,1,0:T(8,128)} %fusion.19, ...), kind=kOutput, calls=%fused_computation.35 | convolution fusion | flops 547356672 | bytes 37880832 | tf_op jit(solution)/shard_map/ok,khw->ohw/dot_general | solution.py:28
  141.5 3.1 %copy.15 = bf16[256,32,128]{2,1,0:T(8,128)(2,1)} copy(bf16[256,32,128]{0,2,1:T(8,128)(2,1)S(1)} %fusion.29) | data formatting | bytes 4194304
  144.5 0.0 all-to-all-done
  144.5 1.8 %gather_fusion = bf16[69,32,128]{2,1,0:T(8,128)(2,1)S(1)} fusion(bf16[96,32,128]{2,1,0:T(8,128)(2,1)} %bitcast.40, s32[1024]{0:T(1024)S(1)} %pad_clamp_fusion), kind=kCustom, calls=%fused_computation | custom fusion | bytes 1130772 | tf_op jit(solution)/shard_map/jit(_take)/gather | solution.py:44
  146.3 1.0 broadcast_select_fusion
  (7 shorter events, 0.1 us)
Async XLA Ops:
  0.6 45.8 %copy-start.1 = (bf16[3,256,512]{2,1,0:T(8,128)(2,1)S(1)}, bf16[3,256,512]{2,1,0:T(8,128)(2,1)}, u32[]{:S(2)}) copy-start(bf16[3,256,512]{2,1,0:T(8,128)(2,1)} %param.8) | copy-start | bytes 2359300
  43.8 12.5 %copy-start.5 = (s32[69]{0:T(128)S(1)}, s32[69]{0:T(128)}, u32[]{:S(2)}) copy-start(s32[69]{0:T(128)} %param.9) | copy-start | bytes 832
  43.9 12.5 %collective-permute-start = (bf16[69,2,128]{0,2,1:T(8,128)(2,1)S(1)}, bf16[69,2,128]{0,2,1:T(8,128)(2,1)S(1)}, u32[]{:S(2)}, u32[]{:S(2)}) collective-permute-start(bf16[69,2,128]{0,2,1:T(8,128)(2,1)S(1)} %get-tuple-element.14), channel_id=1, source_target_pairs={{0,4},{4,8},{8,12},{12,16},{16,20},{20,24},{24,28},{1,5},{5,9},{9,... | collective-permute-start | bytes 105992 | tf_op jit(solution)/shard_map/ppermute | solution.py:14
  45.2 11.2 %collective-permute-start.1 = (bf16[69,2,128]{0,2,1:T(8,128)(2,1)S(1)}, bf16[69,2,128]{0,2,1:T(8,128)(2,1)S(1)}, u32[]{:S(2)}, u32[]{:S(2)}) collective-permute-start(bf16[69,2,128]{0,2,1:T(8,128)(2,1)S(1)} %get-tuple-element.15), channel_id=1, source_target_pairs={{4,0},{8,4},{12,8},{16,12},{20,16},{24,20},{28,24},{5,1},{9,5},{13... | collective-permute-start | bytes 105992 | tf_op jit(solution)/shard_map/ppermute | solution.py:17
  47.7 29.2 %copy-start.2 = (bf16[9,256,69]{1,2,0:T(8,128)(2,1)S(1)}, bf16[9,256,69]{1,2,0:T(8,128)(2,1)}, u32[]{:S(2)}) copy-start(bf16[9,256,69]{1,2,0:T(8,128)(2,1)} %param.10) | copy-start | bytes 953860
  47.7 96.8 %all-to-all-start = ((bf16[32,3,32,128]{3,2,1,0:T(8,128)(2,1)}), bf16[32,3,32,128]{3,2,1,0:T(8,128)(2,1)}, u32[]{:S(2)}, u32[]{:S(2)}) async-start(bf16[32,3,32,128]{3,2,1,0:T(8,128)(2,1)} %bitcast.39), calls=%async_computation | async-start | bytes 1572864 | tf_op jit(solution)/shard_map/all_to_all | solution.py:42
  56.5 20.0 %collective-permute-start.3 = (bf16[69,36,2]{0,2,1:T(2,128)(2,1)S(1)}, bf16[69,36,2]{0,2,1:T(2,128)(2,1)S(1)}, u32[]{:S(2)}, u32[]{:S(2)}) collective-permute-start(bf16[69,36,2]{0,2,1:T(2,128)(2,1)S(1)} %get-tuple-element.13), channel_id=1, source_target_pairs={{1,0},{2,1},{3,2},{0,3},{5,4},{6,5},{7,6},{4,7},{9,8},{10,9},{11,1... | collective-permute-start | bytes 29816 | tf_op jit(solution)/shard_map/ppermute | solution.py:17
  56.8 19.6 %collective-permute-start.2 = (bf16[69,36,2]{0,2,1:T(2,128)(2,1)S(1)}, bf16[69,36,2]{0,2,1:T(2,128)(2,1)S(1)}, u32[]{:S(2)}, u32[]{:S(2)}) collective-permute-start(bf16[69,36,2]{0,2,1:T(2,128)(2,1)S(1)} %get-tuple-element.12), channel_id=1, source_target_pairs={{0,1},{1,2},{2,3},{3,0},{4,5},{5,6},{6,7},{7,4},{8,9},{9,10},{10,1... | collective-permute-start | bytes 29816 | tf_op jit(solution)/shard_map/ppermute | solution.py:14
  95.4 2.9 %copy-start.3 = (f32[256]{0:T(256)S(1)}, f32[256]{0:T(256)}, u32[]{:S(2)}) copy-start(f32[256]{0:T(256)} %param.11) | copy-start | bytes 3076
  98.3 12.7 %copy-start = (bf16[9,256,256]{2,1,0:T(8,128)(2,1)S(1)}, bf16[9,256,256]{2,1,0:T(8,128)(2,1)}, u32[]{:S(2)}) copy-start(bf16[9,256,256]{2,1,0:T(8,128)(2,1)} %param.12) | copy-start | bytes 3538948
  128.0 2.7 %copy-start.4 = (f32[256]{0:T(256)S(1)}, f32[256]{0:T(256)}, u32[]{:S(2)}) copy-start(f32[256]{0:T(256)} %param.13) | copy-start | bytes 3076
where the time goes:
time: 148 us; the launch traced here: 147 us
  matrix products  64.5 us (44%)
  blocking collectives  40.4 us (27%)
  waiting for transfers between devices  17.9 us (12%)
  starting transfers between devices  13.3 us (9%)
  local copies, waits for them, and re-layouts  7.99 us (5%)
  other arithmetic  2.36 us (2%)
    dot_general x18, matrix products, conv_valid(): jnp.einsum('ok,khw->ohw', weight[tap], shifted, preferred_element_type=jn...  64.5 us
    psum x1, blocking collectives, encode(): lax.psum((jnp.sum(values, axis=(1, 2)), jnp.sum(values * values, axis=(1,...  40.4 us
    ppermute x2, waiting for transfers between devices, padded_2(): lax.ppermute(lax.slice_in_dim(block, 0, width, axis=dim), axis, backward)  17.9 us
    all_to_all x1, starting transfers between devices, regrid(): lax.all_to_all(ordered, ('lat', 'lon'), split_axis=0, concat_axis=1, tile...  8.59 us
    unnamed x14, local copies, waits for them, and re-layouts  4.93 us
    ppermute x2, starting transfers between devices, padded_2(): lax.ppermute(lax.slice_in_dim(block, block.shape[dim] - width, None, axis...  3 us
  transfers between devices with their start and end apart: 5, of which 1 were waited for; matrix products, arithmetic and copies ran while one was open for 47% of the time, Pallas kernels for 0%

commit v1 on v0

--- a/solution.py
+++ b/solution.py
@@ -50,7 +50,8 @@
     lon_cols = values.shape[2]
     cells = lat_rows * lax.axis_size("lat") * lon_cols * lax.axis_size("lon")
     total, squares = lax.psum(
-        (jnp.sum(values, axis=(1, 2)), jnp.sum(values * values, axis=(1, 2))), ("lat", "lon")
+        lax.psum((jnp.sum(values, axis=(1, 2)), jnp.sum(values * values, axis=(1, 2))), "lon"),
+        "lat",
     )
     mean = total / cells
     scale = 1.0 / jnp.sqrt(squares / cells - mean * mean + 1e-05)

time: 148 us -> 128 us (0.86)
  blocking collectives: 40.4 us -> 20.9 us
    psum x1, blocking collectives: 40.4 us -> 9 us  [encode(): lax.psum((jnp.sum(values, axis=(1, 2)), jnp.sum(values * values, axis=(1,...]
    psum x0 -> x1, blocking collectives: none -> 11.9 us  [encode(): lax.psum(lax.psum((jnp.sum(values, axis=(1, 2)), jnp.sum(values * values,...]
  transfers between devices with their start and end apart: 5 -> 5, of which waited for: 1 -> 1; matrix products, arithmetic and copies ran while one was open for 47% -> 54% of each run, Pallas kernels for 0% -> 0%
where the time goes in v1:
time: 128 us
  matrix products  64.5 us (50%)
  blocking collectives  20.9 us (16%)
  waiting for transfers between devices  17.9 us (14%)
  starting transfers between devices  13.6 us (11%)
  local copies, waits for them, and re-layouts  8 us (6%)
  other arithmetic  2.36 us (2%)
    dot_general x18, matrix products, conv_valid(): jnp.einsum('ok,khw->ohw', weight[tap], shifted, preferred_element_type=jn...  64.5 us
    ppermute x2, waiting for transfers between devices, padded_2(): lax.ppermute(lax.slice_in_dim(block, 0, width, axis=dim), axis, backward)  17.9 us
    psum x1, blocking collectives, encode(): lax.psum(lax.psum((jnp.sum(values, axis=(1, 2)), jnp.sum(values * values,...  11.9 us
    psum x1, blocking collectives, encode(): lax.psum((jnp.sum(values, axis=(1, 2)), jnp.sum(values * values, axis=(1,...  9 us
    all_to_all x1, starting transfers between devices, regrid(): lax.all_to_all(ordered, ('lat', 'lon'), split_axis=0, concat_axis=1, tile...  8.59 us
    unnamed x14, local copies, waits for them, and re-layouts  4.93 us
    ppermute x2, starting transfers between devices, padded_2(): lax.ppermute(lax.slice_in_dim(block, block.shape[dim] - width, None, axis...  3.33 us
  transfers between devices with their start and end apart: 5, of which 1 were waited for; matrix products, arithmetic and copies ran while one was open for 54% of the time, Pallas kernels for 0%

profile of v1, /device:TPU:8, one launch (start us, length us, event | category | flops | bytes accessed | tf_op | source)
XLA Modules:
  0.0 128.2 jit_solution(5238870986373519348)
XLA Ops:
  0.6 0.0 copy-start.1
  0.6 1.8 %copy.13 = bf16[69,32,128]{0,2,1:T(8,128)(2,1)S(1)} copy(bf16[69,32,128]{2,1,0:T(8,128)(2,1)} %param.7) | data formatting | bytes 1130496 | tf_op args[0]
  2.5 0.6 convert_reduce_fusion
  3.1 9.0 %all-reduce.1 = (f32[69]{0:T(128)S(1)}, f32[69]{0:T(128)S(1)}) all-reduce(f32[69]{0:T(128)S(1)} %get-tuple-element.9, f32[69]{0:T(128)S(1)} %get-tuple-element.8), channel_id=1, replica_groups=mesh['lat'=8,'lon'=4] {'lon'}, use_global_device_ids=true, to_apply=%region_4.0 | all-reduce | flops 138 | bytes 1104 | tf_op jit(solution)/shard_map/psum | solution.py:53
  12.0 11.9 %all-reduce = (f32[69]{0:T(128)S(1)}, f32[69]{0:T(128)S(1)}) all-reduce(f32[69]{0:T(128)S(1)} %get-tuple-element.12, f32[69]{0:T(128)S(1)} %get-tuple-element.13), channel_id=1, replica_groups=mesh['lat'=8,'lon'=4] {'lat'}, use_global_device_ids=true, to_apply=%region_5.0 | all-reduce | flops 138 | bytes 1104 | tf_op jit(solution)/shard_map/psum | solution.py:52
  24.0 0.3 fusion.10
  24.3 0.0 copy-start.5
  24.3 1.6 %collective-permute-start = (bf16[69,2,128]{0,2,1:T(8,128)(2,1)S(1)}, bf16[69,2,128]{0,2,1:T(8,128)(2,1)S(1)}, u32[]{:S(2)}, u32[]{:S(2)}) collective-permute-start(bf16[69,2,128]{0,2,1:T(8,128)(2,1)S(1)} %get-tuple-element.16), channel_id=1, source_target_pairs={{0,4},{4,8},{8,12},{12,16},{16,20},{20,24},{24,28},{1,5},{5,9},{9,... | collective-permute-start | bytes 105992 | tf_op jit(solution)/shard_map/ppermute | solution.py:14
  26.0 1.3 %collective-permute-start.1 = (bf16[69,2,128]{0,2,1:T(8,128)(2,1)S(1)}, bf16[69,2,128]{0,2,1:T(8,128)(2,1)S(1)}, u32[]{:S(2)}, u32[]{:S(2)}) collective-permute-start(bf16[69,2,128]{0,2,1:T(8,128)(2,1)S(1)} %get-tuple-element.17), channel_id=1, source_target_pairs={{4,0},{8,4},{12,8},{16,12},{20,16},{24,20},{28,24},{5,1},{9,5},{13... | collective-permute-start | bytes 105992 | tf_op jit(solution)/shard_map/ppermute | solution.py:17
  27.3 0.0 copy-done.1
  27.3 0.2 reshape.34
  27.5 1.1 copy.14
  28.6 0.0 copy-start.2
  28.6 8.6 %all-to-all-start = ((bf16[32,3,32,128]{3,2,1,0:T(8,128)(2,1)}), bf16[32,3,32,128]{3,2,1,0:T(8,128)(2,1)}, u32[]{:S(2)}, u32[]{:S(2)}) async-start(bf16[32,3,32,128]{3,2,1,0:T(8,128)(2,1)} %bitcast.39), calls=%async_computation | async-start | bytes 1572864 | tf_op jit(solution)/shard_map/all_to_all | solution.py:42
  37.1 0.0 copy-done.5
  37.2 0.0 collective-permute-done
  37.2 0.0 collective-permute-done.1
  37.3 0.4 collective-permute-start.3
  37.6 1.7 %collective-permute-start.2 = (bf16[69,36,2]{0,2,1:T(2,128)(2,1)S(1)}, bf16[69,36,2]{0,2,1:T(2,128)(2,1)S(1)}, u32[]{:S(2)}, u32[]{:S(2)}) collective-permute-start(bf16[69,36,2]{0,2,1:T(2,128)(2,1)S(1)} %get-tuple-element.14), channel_id=1, source_target_pairs={{0,1},{1,2},{2,3},{3,0},{4,5},{5,6},{6,7},{7,4},{8,9},{9,10},{10,1... | collective-permute-start | bytes 29816 | tf_op jit(solution)/shard_map/ppermute | solution.py:14
  39.4 17.9 %collective-permute-done.3 = bf16[69,36,2]{0,2,1:T(2,128)(2,1)S(1)} collective-permute-done((bf16[69,36,2]{0,2,1:T(2,128)(2,1)S(1)}, bf16[69,36,2]{0,2,1:T(2,128)(2,1)S(1)}, u32[]{:S(2)}, u32[]{:S(2)}) %collective-permute-start.3) | collective-permute-done | bytes 9968 | tf_op jit(solution)/shard_map/ppermute | solution.py:17
  57.3 0.0 collective-permute-done.2
  57.3 0.5 pad_maximum_fusion
  57.7 0.0 copy-done.2
  57.7 0.8 fusion.32
  58.5 3.0 %fusion.34 = f32[34,130,256]{2,1,0:T(8,128)} fusion(bf16[69,36,132]{0,2,1:T(8,128)(2,1)S(1)} %pad_maximum_fusion, bf16[9,256,69]{1,2,0:T(8,128)(2,1)S(1)} %copy-done.2), kind=kOutput, calls=%fused_computation.41 | convolution fusion | flops 156149760 | bytes 5746688 | tf_op jit(solution)/shard_map/ok,khw->ohw/dot_general | solution.py:28
  61.5 2.9 %fusion.36 = f32[34,130,256]{2,1,0:T(8,128)} fusion(bf16[69,36,132]{0,2,1:T(8,128)(2,1)S(1)} %pad_maximum_fusion, bf16[9,256,69]{1,2,0:T(8,128)(2,1)S(1)} %copy-done.2), kind=kOutput, calls=%fused_computation.43 | convolution fusion | flops 156149760 | bytes 5746688 | tf_op jit(solution)/shard_map/ok,khw->ohw/dot_general | solution.py:28
  64.4 2.9 %fusion.63 = f32[34,130,256]{2,1,0:T(8,128)} fusion(bf16[9,256,69]{1,2,0:T(8,128)(2,1)S(1)} %copy-done.2, bf16[69,36,2]{0,2,1:T(2,128)(2,1)S(1)} %collective-permute-done.3, bf16[69,2,128]{0,2,1:T(8,128)(2,1)S(1)} %collective-permute-done.1, bf16[69,32,128]{0,2,1:T(8,128)(2,1)S(1)} %fusion.10, bf16[69,2,128]{0,2,1:T(8,128)(2,1)S(1)} %collective-permute-done), kind=kOutput, calls=%fused_computation.69 | convolution fusion | flops 158733120 | bytes 5761024 | tf_op jit(solution)/shard_map/ok,khw->ohw/dot_general | solution.py:28
  67.3 2.9 %fusion.66 = f32[34,130,256]{2,1,0:T(8,128)} fusion(bf16[9,256,69]{1,2,0:T(8,128)(2,1)S(1)} %copy-done.2, bf16[69,2,128]{0,2,1:T(8,128)(2,1)S(1)} %collective-permute-done.1, bf16[69,32,128]{0,2,1:T(8,128)(2,1)S(1)} %fusion.10, bf16[69,2,128]{0,2,1:T(8,128)(2,1)S(1)} %collective-permute-done, bf16[69,36,2]{0,2,1:T(2,128)(2,1)S(1)} %collective-permute-done.2), kind=kOutput, calls=%fused_computation.72 | convolution fusion | flops 158733120 | bytes 5761024 | tf_op jit(solution)/shard_map/ok,khw->ohw/dot_general | solution.py:28
  70.2 2.9 %fusion.68 = f32[34,130,256]{2,1,0:T(8,128)} fusion(bf16[9,256,69]{1,2,0:T(8,128)(2,1)S(1)} %copy-done.2, bf16[69,36,2]{0,2,1:T(2,128)(2,1)S(1)} %collective-permute-done.3, bf16[69,2,128]{0,2,1:T(8,128)(2,1)S(1)} %collective-permute-done.1, bf16[69,32,128]{0,2,1:T(8,128)(2,1)S(1)} %fusion.10, bf16[69,2,128]{0,2,1:T(8,128)(2,1)S(1)} %collective-permute-done), kind=kOutput, calls=%fused_computation.74 | convolution fusion | flops 158733120 | bytes 5761024 | tf_op jit(solution)/shard_map/ok,khw->ohw/dot_general | solution.py:28
  73.2 3.0 %fusion.71 = f32[34,130,256]{2,1,0:T(8,128)} fusion(bf16[9,256,69]{1,2,0:T(8,128)(2,1)S(1)} %copy-done.2, bf16[69,2,128]{0,2,1:T(8,128)(2,1)S(1)} %collective-permute-done.1, bf16[69,32,128]{0,2,1:T(8,128)(2,1)S(1)} %fusion.10, bf16[69,2,128]{0,2,1:T(8,128)(2,1)S(1)} %collective-permute-done, bf16[69,36,2]{0,2,1:T(2,128)(2,1)S(1)} %collective-permute-done.2), kind=kOutput, calls=%fused_computation.77 | convolution fusion | flops 158733120 | bytes 5761024 | tf_op jit(solution)/shard_map/ok,khw->ohw/dot_general | solution.py:28
  76.2 0.0 copy-start.3
  76.2 2.9 %fusion.61 = f32[34,130,256]{2,1,0:T(8,128)} fusion(bf16[9,256,69]{1,2,0:T(8,128)(2,1)S(1)} %copy-done.2, bf16[69,2,128]{0,2,1:T(8,128)(2,1)S(1)} %collective-permute-done.1, bf16[69,32,128]{0,2,1:T(8,128)(2,1)S(1)} %fusion.10, bf16[69,2,128]{0,2,1:T(8,128)(2,1)S(1)} %collective-permute-done, bf16[69,36,2]{0,2,1:T(2,128)(2,1)S(1)} %collective-permute-done.2), kind=kOutput, calls=%fused_computation.67 | convolution fusion | flops 158733120 | bytes 5761024 | tf_op jit(solution)/shard_map/ok,khw->ohw/dot_general | solution.py:28
  79.1 0.0 copy-done.3
  79.1 0.0 copy-start
  79.1 12.7 %fusion.8 = bf16[256,34,130]{0,2,1:T(8,128)(2,1)S(1)} fusion(f32[34,130,256]{2,1,0:T(8,128)S(1)} %fusion.32, f32[34,130,256]{2,1,0:T(8,128)} %fusion.61, f32[34,130,256]{2,1,0:T(8,128)} %fusion.63, f32[34,130,256]{2,1,0:T(8,128)} %fusion.34, f32[34,130,256]{2,1,0:T(8,128)} %fusion.66, f32[34,130,256]{2,1,0:T(8,128)} %fusion.68, ...), kind=kOutput, calls=%fused_computation.10 | convolution fusion | flops 180232000 | bytes 39917056 | tf_op jit(solution)/shard_map/ok,khw->ohw/dot_general | solution.py:28
  91.8 0.0 copy-done
  91.8 0.8 fusion.13
  92.6 2.7 %fusion.15 = f32[32,128,256]{2,1,0:T(8,128)} fusion(bf16[256,34,130]{0,2,1:T(8,128)(2,1)S(1)} %fusion.8, bf16[9,256,256]{2,1,0:T(8,128)(2,1)S(1)} %copy-done), kind=kOutput, calls=%fused_computation.21 | convolution fusion | flops 536870912 | bytes 6422528 | tf_op jit(solution)/shard_map/ok,khw->ohw/dot_general | solution.py:28
  95.3 2.7 %fusion.17 = f32[32,128,256]{2,1,0:T(8,128)} fusion(bf16[256,34,130]{0,2,1:T(8,128)(2,1)S(1)} %fusion.8, bf16[9,256,256]{2,1,0:T(8,128)(2,1)S(1)} %copy-done), kind=kOutput, calls=%fused_computation.23 | convolution fusion | flops 536870912 | bytes 6422528 | tf_op jit(solution)/shard_map/ok,khw->ohw/dot_general | solution.py:28
  98.0 2.7 %fusion.19 = f32[32,128,256]{2,1,0:T(8,128)} fusion(bf16[256,34,130]{0,2,1:T(8,128)(2,1)S(1)} %fusion.8, bf16[9,256,256]{2,1,0:T(8,128)(2,1)S(1)} %copy-done), kind=kOutput, calls=%fused_computation.25 | convolution fusion | flops 536870912 | bytes 6422528 | tf_op jit(solution)/shard_map/ok,khw->ohw/dot_general | solution.py:28
  100.7 2.7 %fusion.21 = f32[32,128,256]{2,1,0:T(8,128)} fusion(bf16[256,34,130]{0,2,1:T(8,128)(2,1)S(1)} %fusion.8, bf16[9,256,256]{2,1,0:T(8,128)(2,1)S(1)} %copy-done), kind=kOutput, calls=%fused_computation.27 | convolution fusion | flops 536870912 | bytes 6422528 | tf_op jit(solution)/shard_map/ok,khw->ohw/dot_general | solution.py:28
  103.4 2.7 %fusion.23 = f32[32,128,256]{2,1,0:T(8,128)} fusion(bf16[256,34,130]{0,2,1:T(8,128)(2,1)S(1)} %fusion.8, bf16[9,256,256]{2,1,0:T(8,128)(2,1)S(1)} %copy-done), kind=kOutput, calls=%fused_computation.29 | convolution fusion | flops 536870912 | bytes 6422528 | tf_op jit(solution)/shard_map/ok,khw->ohw/dot_general | solution.py:28
  106.1 2.7 %fusion.25 = f32[32,128,256]{2,1,0:T(8,128)} fusion(bf16[256,34,130]{0,2,1:T(8,128)(2,1)S(1)} %fusion.8, bf16[9,256,256]{2,1,0:T(8,128)(2,1)S(1)} %copy-done), kind=kOutput, calls=%fused_computation.31 | convolution fusion | flops 536870912 | bytes 6422528 | tf_op jit(solution)/shard_map/ok,khw->ohw/dot_general | solution.py:28
  108.8 0.0 copy-start.4
  108.8 2.7 %fusion.27 = f32[32,128,256]{2,1,0:T(8,128)} fusion(bf16[256,34,130]{0,2,1:T(8,128)(2,1)S(1)} %fusion.8, bf16[9,256,256]{2,1,0:T(8,128)(2,1)S(1)} %copy-done), kind=kOutput, calls=%fused_computation.33 | convolution fusion | flops 536870912 | bytes 6422528 | tf_op jit(solution)/shard_map/ok,khw->ohw/dot_general | solution.py:28
  111.6 0.0 copy-done.4
  111.6 10.8 %fusion.29 = bf16[256,32,128]{0,2,1:T(8,128)(2,1)S(1)} fusion(f32[256]{0:T(256)S(1)} %copy-done.4, bf16[256,34,130]{0,2,1:T(8,128)(2,1)S(1)} %fusion.8, f32[32,128,256]{2,1,0:T(8,128)S(1)} %fusion.13, f32[32,128,256]{2,1,0:T(8,128)} %fusion.15, f32[32,128,256]{2,1,0:T(8,128)} %fusion.17, f32[32,128,256]{2,1,0:T(8,128)} %fusion.19, ...), kind=kOutput, calls=%fused_computation.35 | convolution fusion | flops 547356672 | bytes 37880832 | tf_op jit(solution)/shard_map/ok,khw->ohw/dot_general | solution.py:28
  122.3 3.1 %copy.15 = bf16[256,32,128]{2,1,0:T(8,128)(2,1)} copy(bf16[256,32,128]{0,2,1:T(8,128)(2,1)S(1)} %fusion.29) | data formatting | bytes 4194304
  125.4 0.0 all-to-all-done
  125.4 1.8 %gather_fusion = bf16[69,32,128]{2,1,0:T(8,128)(2,1)S(1)} fusion(bf16[96,32,128]{2,1,0:T(8,128)(2,1)} %bitcast.40, s32[1024]{0:T(1024)S(1)} %pad_clamp_fusion), kind=kCustom, calls=%fused_computation | custom fusion | bytes 1130772 | tf_op jit(solution)/shard_map/jit(_take)/gather | solution.py:44
  127.2 1.0 broadcast_select_fusion
  (7 shorter events, 0.1 us)
Async XLA Ops:
  0.6 26.6 %copy-start.1 = (bf16[3,256,512]{2,1,0:T(8,128)(2,1)S(1)}, bf16[3,256,512]{2,1,0:T(8,128)(2,1)}, u32[]{:S(2)}) copy-start(bf16[3,256,512]{2,1,0:T(8,128)(2,1)} %param.8) | copy-start | bytes 2359300
  24.3 12.8 %copy-start.5 = (s32[69]{0:T(128)S(1)}, s32[69]{0:T(128)}, u32[]{:S(2)}) copy-start(s32[69]{0:T(128)} %param.9) | copy-start | bytes 832
  24.3 12.9 %collective-permute-start = (bf16[69,2,128]{0,2,1:T(8,128)(2,1)S(1)}, bf16[69,2,128]{0,2,1:T(8,128)(2,1)S(1)}, u32[]{:S(2)}, u32[]{:S(2)}) collective-permute-start(bf16[69,2,128]{0,2,1:T(8,128)(2,1)S(1)} %get-tuple-element.16), channel_id=1, source_target_pairs={{0,4},{4,8},{8,12},{12,16},{16,20},{20,24},{24,28},{1,5},{5,9},{9,... | collective-permute-start | bytes 105992 | tf_op jit(solution)/shard_map/ppermute | solution.py:14
  26.0 11.2 %collective-permute-start.1 = (bf16[69,2,128]{0,2,1:T(8,128)(2,1)S(1)}, bf16[69,2,128]{0,2,1:T(8,128)(2,1)S(1)}, u32[]{:S(2)}, u32[]{:S(2)}) collective-permute-start(bf16[69,2,128]{0,2,1:T(8,128)(2,1)S(1)} %get-tuple-element.17), channel_id=1, source_target_pairs={{4,0},{8,4},{12,8},{16,12},{20,16},{24,20},{28,24},{5,1},{9,5},{13... | collective-permute-start | bytes 105992 | tf_op jit(solution)/shard_map/ppermute | solution.py:17
  28.6 29.2 %copy-start.2 = (bf16[9,256,69]{1,2,0:T(8,128)(2,1)S(1)}, bf16[9,256,69]{1,2,0:T(8,128)(2,1)}, u32[]{:S(2)}) copy-start(bf16[9,256,69]{1,2,0:T(8,128)(2,1)} %param.10) | copy-start | bytes 953860
  28.6 96.8 %all-to-all-start = ((bf16[32,3,32,128]{3,2,1,0:T(8,128)(2,1)}), bf16[32,3,32,128]{3,2,1,0:T(8,128)(2,1)}, u32[]{:S(2)}, u32[]{:S(2)}) async-start(bf16[32,3,32,128]{3,2,1,0:T(8,128)(2,1)} %bitcast.39), calls=%async_computation | async-start | bytes 1572864 | tf_op jit(solution)/shard_map/all_to_all | solution.py:42
  37.3 20.0 %collective-permute-start.3 = (bf16[69,36,2]{0,2,1:T(2,128)(2,1)S(1)}, bf16[69,36,2]{0,2,1:T(2,128)(2,1)S(1)}, u32[]{:S(2)}, u32[]{:S(2)}) collective-permute-start(bf16[69,36,2]{0,2,1:T(2,128)(2,1)S(1)} %get-tuple-element.15), channel_id=1, source_target_pairs={{1,0},{2,1},{3,2},{0,3},{5,4},{6,5},{7,6},{4,7},{9,8},{10,9},{11,1... | collective-permute-start | bytes 29816 | tf_op jit(solution)/shard_map/ppermute | solution.py:17
  37.6 19.6 %collective-permute-start.2 = (bf16[69,36,2]{0,2,1:T(2,128)(2,1)S(1)}, bf16[69,36,2]{0,2,1:T(2,128)(2,1)S(1)}, u32[]{:S(2)}, u32[]{:S(2)}) collective-permute-start(bf16[69,36,2]{0,2,1:T(2,128)(2,1)S(1)} %get-tuple-element.14), channel_id=1, source_target_pairs={{0,1},{1,2},{2,3},{3,0},{4,5},{5,6},{6,7},{7,4},{8,9},{9,10},{10,1... | collective-permute-start | bytes 29816 | tf_op jit(solution)/shard_map/ppermute | solution.py:14
  76.2 2.9 %copy-start.3 = (f32[256]{0:T(256)S(1)}, f32[256]{0:T(256)}, u32[]{:S(2)}) copy-start(f32[256]{0:T(256)} %param.11) | copy-start | bytes 3076
  79.1 12.7 %copy-start = (bf16[9,256,256]{2,1,0:T(8,128)(2,1)S(1)}, bf16[9,256,256]{2,1,0:T(8,128)(2,1)}, u32[]{:S(2)}) copy-start(bf16[9,256,256]{2,1,0:T(8,128)(2,1)} %param.12) | copy-start | bytes 3538948
  108.8 2.7 %copy-start.4 = (f32[256]{0:T(256)S(1)}, f32[256]{0:T(256)}, u32[]{:S(2)}) copy-start(f32[256]{0:T(256)} %param.13) | copy-start | bytes 3076
